TPU v7x, 32 devices: a whole 2x2x4 slice. The times are simulated.
32 devices in a mesh: lon: 8 (over y, x, core), lat: 4 (over z).
Axes of the slice: x: 2, y: 2, z: 4, core: 2. Of those that a mesh axis runs over, the one named last changes fastest.
Arguments:
- height_old: float32 [1024, 512], P('lon', 'lat'), may hold values from -6 to 6
- height_now: float32 [1024, 512], P('lon', 'lat'), may hold values from -6 to 6
- zonal_old: float32 [1024, 512], P('lon', 'lat'), may hold values from -6 to 6
- zonal_now: float32 [1024, 512], P('lon', 'lat'), may hold values from -6 to 6
- meridional_old: float32 [1024, 512], P('lon', 'lat'), may hold values from -6 to 6
- meridional_now: float32 [1024, 512], P('lon', 'lat'), may hold values from -6 to 6
- ocean_depth: float32 [1024, 512], P('lon', 'lat'), may hold values from 0.2 to 1
- land_sea: int32 [1024, 512], P('lon', 'lat'), may hold values 0 or 1
- metric_factor: float32 [512], P('lat'), may hold values from 0.5 to 2
- coriolis: float32 [512], P('lat'), may hold values from -0.5 to 0.5
- implicit_weight: float32 [512], replicated, may hold values from 150 to 40000
- source_longitude: int32 [512], replicated, may hold values from 0 to 1023
- source_latitude: int32 [512], replicated, may hold values from 0 to 511
- source_amplitude: float32 [512], replicated, may hold values from -24 to 24
Outputs:
- height_final: float32 [1024, 512], P('lon', 'lat')
- zonal_final: float32 [1024, 512], P('lon', 'lat')
- meridional_final: float32 [1024, 512], P('lon', 'lat')
Inputs may be any that keep to these rules, and one draw needn't show every extreme that they name: `source_longitude`: cells may repeat.
All inputs are finite; a program needn't handle non-finite values. No bound on the sum of `land_sea` on one device may be relied on, other than what follows from the above.
Results may differ from a plain program's by a relative error of at most 0.0003.
Values sent between devices are 32-bit elements; how exact they have to be, the bound alone decides.
A program may use at most 64 MiB of HBM per device.

v0:
```python
import functools

import jax
import jax.numpy as jnp
from jax import lax
from jax.experimental import pallas as pl
from jax.experimental.pallas import tpu as pltpu
from jax.sharding import PartitionSpec as P

COURANT = 0.25
MESH = pl.DeviceIdType.MESH
HIGHEST = lax.Precision.HIGHEST
LAST_WITH_LAST = (((1,), (1,)), ((), ()))
FIRST_WITH_FIRST = (((0,), (0,)), ((), ()))
PLAIN = (((1,), (0,)), ((), ()))
WINDOW = 16
STRIDES = 8


def exact_dot(left, right, dims):
    return lax.dot_general(left, right, dims, precision=HIGHEST, preferred_element_type=jnp.float32)


def pieces(value):
    found = []
    for _ in range(3):
        piece = value.astype(jnp.bfloat16).astype(jnp.float32)
        found.append(piece)
        value = value - piece
    return found


def line_scan(a, lane, upward):
    rows = a.shape[1]
    one, zero = jnp.ones_like(a), jnp.zeros_like(a)

    def behind(v, amount):
        return pltpu.roll(v, amount if upward else rows - amount, 1)

    def inside(amount):
        return lane >= amount if upward else lane < rows - amount

    window = min(WINDOW, rows)
    m = [one, zero, zero, one]
    for i in range(window - 1, -1, -1):
        step = behind(a, i) if i else a
        keep = inside(i)
        for x, y in ((0, 2), (1, 3)):
            total = m[x] + m[y]
            grown = m[x] + step * total
            m[x] = jnp.where(keep, grown, m[x]) if i else grown
            m[y] = jnp.where(keep, total, m[y]) if i else total
    unit = (1.0, 0.0, 0.0, 1.0)
    while window < rows:
        count = min(STRIDES, rows // window)
        terms = [m]
        for i in range(1, count):
            keep = inside(i * window)
            terms.append([jnp.where(keep, behind(v, i * window), u) for v, u in zip(m, unit)])
        while len(terms) > 1:
            joined = []
            for p, q in zip(terms[0::2], terms[1::2]):
                joined.append(
                    [
                        p[0] * q[0] + p[1] * q[2],
                        p[0] * q[1] + p[1] * q[3],
                        p[2] * q[0] + p[3] * q[2],
                        p[2] * q[1] + p[3] * q[3],
                    ]
                )
            terms = joined + terms[2 * len(joined) :]
        m = terms[0]
        window *= count
    return m


def line_factors(a, up, down, before, after, blocks):
    padded, rows = a.shape
    one = jnp.ones_like(a)

    def carried(m, edge, order):
        m = [jnp.broadcast_to(v[:, edge : edge + 1], (padded, rows)) for v in m]
        x, y = one[:1], jnp.zeros_like(one[:1])
        xs, ys, shrink = {}, {}, {}
        for c in order:
            xs[c], ys[c] = x, y
            nx = m[0][c : c + 1] * x + m[1][c : c + 1] * y
            ny = m[2][c : c + 1] * x + m[3][c : c + 1] * y
            ratio = 1.0 / (nx + ny)
            shrink[c] = ratio
            x, y = nx * ratio, ny * ratio
        spare = [one[:1]] * (padded - blocks)
        return [jnp.concatenate([t[c] for c in range(blocks)] + spare, axis=0) for t in (xs, ys, shrink)]

    x_in, y_in, shrink_up = carried(up, rows - 1, range(blocks))
    xb_in, yb_in, shrink_down = carried(down, 0, range(blocks - 1, -1, -1))
    x = up[0] * x_in + up[1] * y_in
    y = up[2] * x_in + up[3] * y_in
    yb = down[2] * xb_in + down[3] * yb_in
    end = lambda v: jnp.broadcast_to(v[:, rows - 1 :], (padded, rows))
    scale = 1.0 / (end(x) + end(y) * xb_in)
    return (
        a * y,
        a * yb,
        y * scale,
        yb * scale,
        shrink_up,
        shrink_down,
        x_in,
        y_in,
        xb_in,
        yb_in,
        -before * y_in,
        after * yb_in,
    )


def kernel(lons, lats, *refs):
    ins, outs, refs = refs[:14], refs[14:17], refs[17:]
    (
        fields,
        land,
        pair,
        wgt,
        slon,
        slat,
        amp,
        load_sem,
        factors,
        starts,
        send_lat,
        send_side,
        send_next,
        recv_lat,
        recv_side,
        recv_next,
        send_sem,
        recv_sem,
    ) = refs
    a_id = lax.axis_index("lon")
    b_id = lax.axis_index("lat")
    sides = (lax.rem(a_id + lons - 1, lons), lax.rem(a_id + 1, lons))
    znow, depth, hnow, mnow, hold, zold, mold = (fields.at[k] for k in range(7))
    met, cor, samp = pair.at[0], pair.at[1], amp.at[0]
    columns, rows = land.shape
    padded = wgt.shape[0]

    barrier = pltpu.get_barrier_semaphore()
    for group, number, to in (
        (0, 3, znow),
        (0, 6, depth),
        (0, 7, land),
        (0, 1, hnow),
        (1, 8, met),
        (1, 9, cor),
        (2, 10, wgt.at[pl.ds(0, lats)]),
        (3, 5, mnow),
        (3, 0, hold),
        (4, 11, slon),
        (4, 12, slat),
        (4, 13, samp),
        (3, 2, zold),
        (3, 4, mold),
    ):
        pltpu.make_async_copy(ins[number], to, load_sem.at[group]).start()

    def loaded(group, ref):
        pltpu.make_async_copy(ref, ref, load_sem.at[group]).wait()

    for k in range(1, lats):
        other = lax.rem(b_id + k, lats)
        for column in (*sides, a_id):
            pl.semaphore_signal(barrier, inc=1, device_id=(column, other), device_id_type=MESH)
    for side in sides:
        pl.semaphore_signal(barrier, inc=1, device_id=(side, b_id), device_id_type=MESH)

    loaded(0, fields.at[pl.ds(0, 4)])
    loaded(1, pair)
    scaled_metric = COURANT * met[...]
    for side, (at, sign) in enumerate(((0, -1.0), (columns - 1, 1.0))):
        edge = pl.ds(at, 1)
        flux = depth[edge, :] * land[edge, :].astype(jnp.float32) * znow[edge, :]
        flux = sign * scaled_metric * flux
        send_side[side] = flux
        send_next[side] = jnp.concatenate([flux, hnow[edge, :]], axis=0)

    def remote(src, dst, kind, column, row):
        return pltpu.make_async_remote_copy(
            src_ref=src,
            dst_ref=dst,
            send_sem=send_sem.at[kind],
            recv_sem=recv_sem.at[kind],
            device_id=(column, row),
            device_id_type=MESH,
        )

    def greet_and_send_edges():
        pl.semaphore_wait(barrier, 3 * lats - 1)
        for k in range(1, lats):
            for side in (1, 0):
                remote(
                    send_side.at[side],
                    recv_side.at[side, lats - k - 1],
                    0,
                    sides[side],
                    lax.rem(b_id + k, lats),
                ).start()
        for side in (0, 1):
            remote(send_next.at[side], recv_next.at[side], 1, sides[side], b_id).start()

    far = jnp.logical_and(b_id == lats - 1, a_id > 1)
    pl.when(far)(greet_and_send_edges)

    loaded(2, wgt.at[pl.ds(0, lats)])
    weight = wgt[...]
    if padded > lats:
        row_id = lax.broadcasted_iota(jnp.int32, (padded, rows), 0)
        weight = jnp.where(row_id < lats, weight, 1.0)
    a = 1.0 / weight
    lane_of = lax.broadcasted_iota(jnp.int32, (padded, rows), 1)
    first_lane, last_lane = lane_of == 0, lane_of == rows - 1
    before = COURANT * pltpu.roll(jnp.broadcast_to(a[:, rows - 1 :], (padded, rows)), 1, 0)
    after = COURANT * pltpu.roll(jnp.broadcast_to(a[:, :1], (padded, rows)), padded - 1, 0)
    up = line_scan(a, lane_of, True)
    down = line_scan(a, lane_of, False)
    zeros = jnp.zeros_like(a)
    at_last = lambda v: jnp.where(last_lane, v, zeros)
    at_first = lambda v: jnp.where(first_lane, v, zeros)
    for k, value in enumerate(
        (
            a * up[2],
            a * up[3],
            a * down[2],
            a * down[3],
            at_last((up[0] + up[2]) * after),
            at_last((up[1] + up[3]) * after) - at_first(before),
            -at_first((down[0] + down[2]) * before),
            at_last(after) - at_first((down[1] + down[3]) * before),
        )
    ):
        starts[k] = value

    loaded(3, fields.at[pl.ds(3, 4)])
    loaded(4, amp)
    wet = land[...].astype(jnp.float32)
    wet_depth = depth[...] * wet
    flux_east = wet_depth * znow[...]
    flux_north = wet_depth * mnow[...]
    metric = met[...]
    line = lax.broadcasted_iota(jnp.int32, (columns, rows), 0)
    lane = lax.broadcasted_iota(jnp.int32, (columns, rows), 1)

    def inner_diff(v, axis, position, size):
        ahead = jnp.where(position == size - 1, 0.0, pltpu.roll(v, size - 1, axis))
        behind = jnp.where(position == 0, 0.0, pltpu.roll(v, 1, axis))
        return ahead - behind

    rhs = hold[...] - COURANT * (
        metric * inner_diff(flux_east, 0, line, columns) + inner_diff(flux_north, 1, lane, rows)
    )
    sources = slon.shape[1]
    east_cell = lax.broadcasted_iota(jnp.int32, (columns, sources), 0) + a_id * columns
    north_cell = lax.broadcasted_iota(jnp.int32, (rows, sources), 0) + b_id * rows
    hit_east = jnp.where(east_cell == slon[...], 1.0, 0.0).astype(jnp.bfloat16)
    hit_north = north_cell == slat[...]
    for piece in pieces(samp[...]):
        rhs = rhs + lax.dot_general(
            hit_east,
            jnp.where(hit_north, piece, 0.0).astype(jnp.bfloat16),
            LAST_WITH_LAST,
            preferred_element_type=jnp.float32,
        )

    height = hnow[...]
    row_lane = lax.broadcasted_iota(jnp.int32, (1, rows), 1)
    first_row = jnp.where(row_lane == 0, 1.0, 0.0)
    last_row = jnp.where(row_lane == rows - 1, 1.0, 0.0)
    zero_row = jnp.zeros((1, rows), jnp.float32)
    outer = exact_dot(
        jnp.concatenate([zero_row, zero_row, last_row, zero_row] + [zero_row] * 2 + [first_row, zero_row], axis=0),
        height,
        LAST_WITH_LAST,
    )
    ends = exact_dot(
        jnp.concatenate([first_row, last_row] + [zero_row] * 6, axis=0), flux_north, LAST_WITH_LAST
    )

    def start(k):
        return starts[k, pl.ds(b_id, 1), :]

    def laid(k):
        return jnp.concatenate(
            [start(k), start(k + 1), zero_row, zero_row, start(k + 2), start(k + 3), zero_row, zero_row], axis=0
        )

    moments = outer + exact_dot(
        jnp.concatenate([laid(0), laid(4)], axis=1),
        jnp.concatenate([rhs, flux_north], axis=1),
        LAST_WITH_LAST,
    )
    send_lat[0] = moments[0:4]
    send_lat[1] = moments[4:8]
    pl.when(jnp.logical_not(far))(greet_and_send_edges)
    for k in range(1, lats):
        remote(
            send_lat.at[jnp.where(b_id + k < lats, 0, 1)],
            recv_lat.at[lats - k - 1],
            2,
            a_id,
            lax.rem(b_id + k, lats),
        ).start()

    for k, value in enumerate(line_factors(a, up, down, before, after, lats)):
        factors[k] = value

    def own(k, block):
        return factors[k, pl.ds(block, 1), :]

    ay, ayb, y_s, yb_s = [own(k, b_id) for k in range(4)]
    columns_of = jnp.transpose(jnp.concatenate([ay, ayb] + [zero_row] * 6, axis=0))
    source_lat = lax.broadcasted_iota(jnp.int32, (rows, rows), 0)
    target_lat = lax.broadcasted_iota(jnp.int32, (rows, rows), 1)
    below = source_lat <= target_lat
    inverse = jnp.where(below, columns_of[:, 0:1] * yb_s, columns_of[:, 1:2] * y_s)
    outs[0][...] = exact_dot(rhs, inverse, PLAIN)
    turning = cor[...]
    outs[1][...] = wet * (
        zold[...] + turning * mnow[...] - COURANT * metric * inner_diff(height, 0, line, columns)
    )
    outs[2][...] = mold[...] - COURANT * inner_diff(height, 1, lane, rows) - turning * znow[...]

    def across(v):
        return v[:, :columns] if columns <= rows else jnp.broadcast_to(v[:, :1], (1, columns))

    coarse, fine, reach = [None] * lats, [None] * lats, [None] * lats
    product = jnp.ones((1, rows), jnp.float32)
    for d in range(lats - 1, 0, -1):
        block = lax.rem(b_id + d, lats)
        product = product * own(4, block)
        coarse[d], fine[d], reach[d] = own(6, block) * product, own(7, block) * product, own(0, block) * product
    product = jnp.ones((1, rows), jnp.float32)
    for d in range(1, lats):
        block = lax.rem(b_id + d, lats)
        north = b_id + d < lats
        product = product * own(5, block)
        coarse[d] = jnp.where(north, own(8, block) * product, coarse[d])
        fine[d] = jnp.where(north, own(9, block) * product, fine[d])
        reach[d] = jnp.where(north, own(1, block) * product, reach[d])
    own_low = across(own(10, b_id)) * ends[0:1]
    own_high = across(own(11, b_id)) * ends[1:2]
    basis = pieces(
        jnp.concatenate(
            [
                jnp.concatenate([yb_s, y_s] + [zero_row] * 6, axis=0),
                jnp.concatenate([zero_row, zero_row, COURANT * first_row, -COURANT * last_row] + [zero_row] * 4, axis=0),
            ],
            axis=1,
        )
    )
    basis = jnp.concatenate([basis[k] for k in (0, 1, 2, 0, 1, 0)], axis=0).astype(jnp.bfloat16)
    full = jnp.ones((rows, rows), jnp.float32)
    lower = jnp.where(below, 1.0, 0.0)
    running = jnp.concatenate(
        [jnp.concatenate([lower, full], axis=0), jnp.concatenate([1.0 - lower, full], axis=0)], axis=1
    ).astype(jnp.bfloat16)

    arrivals = ((2, recv_lat), (1, recv_next), (0, recv_side))
    for kind, ref in arrivals:
        remote(ref, ref, kind, sides[0], b_id).wait_recv()

    low, high = own_low, own_high
    for d in range(1, lats):
        arrived = recv_lat[d - 1, 0:1] * across(coarse[d]) + recv_lat[d - 1, 1:2] * across(fine[d])
        north = b_id + d < lats
        high = high + jnp.where(north, arrived, 0.0)
        low = low + jnp.where(north, 0.0, arrived)
    south_height = jnp.where(b_id > 0, recv_lat[lats - 2, 2:3], 0.0)
    north_height = jnp.where(b_id < lats - 1, recv_lat[0, 2:3], 0.0)
    carried = pieces(
        jnp.concatenate([low, high, south_height, north_height, jnp.zeros((4, columns), jnp.float32)], axis=0)
    )
    carried = jnp.concatenate([carried[k] for k in (0, 0, 0, 1, 1, 2)], axis=0).astype(jnp.bfloat16)
    corrections = lax.dot_general(carried, basis, FIRST_WITH_FIRST, preferred_element_type=jnp.float32)

    lows, highs = [], []
    for side in (1, 0):
        flux = recv_next[side, 0:1]
        low, high = zero_row, zero_row
        for d in range(1, lats):
            arrived = recv_side[side, d - 1] * reach[d]
            north = b_id + d < lats
            high = high + jnp.where(north, arrived, 0.0)
            low = low + jnp.where(north, 0.0, arrived)
        lows.append(jnp.concatenate([flux * ay, low], axis=1))
        highs.append(jnp.concatenate([flux * ayb, high], axis=1))
    spare = jnp.zeros((4, 2 * rows), jnp.float32)
    edges = jnp.concatenate(pieces(jnp.concatenate(lows + highs + [spare], axis=0)), axis=0)
    edges = jnp.concatenate([edges, jnp.zeros((8, 2 * rows), jnp.float32)], axis=0).astype(jnp.bfloat16)
    edges = lax.dot_general(edges, running, PLAIN, preferred_element_type=jnp.float32)
    edges = edges[0:8] + edges[8:16] + edges[16:24]

    solved = outs[0][...] + corrections[:, :rows]
    outs[0][...] = wet * solved
    outs[2][...] = wet * (outs[2][...] + corrections[:, rows:])
    for k, (at, side, sign) in enumerate(((0, 1, COURANT), (columns - 1, 0, -COURANT))):
        edge = pl.ds(at, 1)
        outs[0][edge, :] = wet[at : at + 1] * (
            solved[at : at + 1] + edges[k : k + 1, :rows] * yb_s + edges[2 + k : 3 + k, rows:] * y_s
        )
        outs[1][edge, :] = outs[1][edge, :] + wet[at : at + 1] * (sign * metric * recv_next[side, 1:2])
    for kind, ref in arrivals:
        remote(ref, ref, kind, sides[0], b_id).wait_send()


def store_kernel(*refs):
    stores = [
        pltpu.make_async_copy(refs[k], refs[3 + k], refs[6].at[k]) for k in range(3)
    ]
    for store in stores:
        store.start()
    for store in stores:
        store.wait()


def per_device(lons, lats, *args):
    args = list(args)
    columns, rows = args[0].shape
    sources = args[11].shape[0]
    padded = -(-lats // 8) * 8
    args[8] = args[8].reshape(1, rows)
    args[9] = args[9].reshape(1, rows)
    args[10] = args[10].reshape(lats, rows)
    for k in (11, 12, 13):
        args[k] = args[k].reshape(1, sources)
    out = pltpu.VMEM((columns, rows), jnp.float32)
    others = lats - 1
    results = pl.pallas_call(
        functools.partial(kernel, lons, lats),
        out_shape=(out, out, out),
        in_specs=[pl.BlockSpec(memory_space=pl.ANY)] * 14,
        out_specs=(pl.BlockSpec(memory_space=pltpu.VMEM),) * 3,
        scratch_shapes=[
            pltpu.VMEM((7, columns, rows), jnp.float32),
            pltpu.VMEM((columns, rows), jnp.int32),
            pltpu.VMEM((2, 1, rows), jnp.float32),
            pltpu.VMEM((padded, rows), jnp.float32),
            pltpu.VMEM((1, sources), jnp.int32),
            pltpu.VMEM((1, sources), jnp.int32),
            pltpu.VMEM((3, 1, sources), jnp.float32),
            pltpu.SemaphoreType.DMA((5,)),
            pltpu.VMEM((12, padded, rows), jnp.float32),
            pltpu.VMEM((8, padded, rows), jnp.float32),
            pltpu.VMEM((2, 4, columns), jnp.float32),
            pltpu.VMEM((2, 1, rows), jnp.float32),
            pltpu.VMEM((2, 2, rows), jnp.float32),
            pltpu.VMEM((others, 4, columns), jnp.float32),
            pltpu.VMEM((2, others, 1, rows), jnp.float32),
            pltpu.VMEM((2, 2, rows), jnp.float32),
            pltpu.SemaphoreType.DMA((3,)),
            pltpu.SemaphoreType.DMA((3,)),
        ],
        compiler_params=pltpu.CompilerParams(collective_id=0, has_side_effects=True),
    )(*args)
    return pl.pallas_call(
        store_kernel,
        out_shape=(jax.ShapeDtypeStruct((columns, rows), jnp.float32),) * 3,
        in_specs=[pl.BlockSpec(memory_space=pltpu.VMEM)] * 3,
        out_specs=(pl.BlockSpec(memory_space=pl.ANY),) * 3,
        scratch_shapes=[pltpu.SemaphoreType.DMA((3,))],
    )(*[pltpu.with_memory_space_constraint(r, pltpu.VMEM) for r in results])


def solution(mesh):
    field = P("lon", "lat")
    placed = (field,) * 8 + (P("lat"),) * 2 + (P(),) * 4
    return jax.shard_map(
        functools.partial(per_device, mesh.shape["lon"], mesh.shape["lat"]),
        mesh=mesh,
        in_specs=placed,
        out_specs=(field,) * 3,
        check_vma=False,
    )
```

profile of v0, /device:TPU:0, one launch (start us, length us, event | category | flops | bytes accessed | tf_op | source)
XLA Modules:
  0.0 10.4 jit_solution(10665266806791875849)
XLA Ops:
  0.6 9.1 %shard_map.157 = (f32[128,128]{1,0:T(8,128)S(1)}, f32[128,128]{1,0:T(8,128)S(1)}, f32[128,128]{1,0:T(8,128)S(1)}) custom-call(f32[128,128]{1,0:T(8,128)} %refs_0_.1, f32[128,128]{1,0:T(8,128)} %refs_1_.1, f32[128,128]{1,0:T(8,128)} %refs_2_.1, f32[128,128]{1,0:T(8,128)} %refs_3_.1, f32[128,128]{1,0:T(8,128)} %refs_4_.1, f32[128,128]{1,0:T(8,128)} %refs_5_.1, ...), custom_call_target="tpu_custom_call" | custom-call | tf_op jit(solution)/shard_map/pallas_call | solution.py:437
  9.7 0.7 %shard_map.158 = (f32[128,128]{1,0:T(8,128)}, f32[128,128]{1,0:T(8,128)}, f32[128,128]{1,0:T(8,128)}) custom-call(f32[128,128]{1,0:T(8,128)S(1)} %get-tuple-element.6.refs_0_, f32[128,128]{1,0:T(8,128)S(1)} %get-tuple-element.7.refs_1_, f32[128,128]{1,0:T(8,128)S(1)} %get-tuple-element.8.refs_2_), custom_call_target="tpu_custom_call" | custom-call | tf_op jit(solution)/shard_map/pallas_call | solution.py:464
where the time goes:
time: 10.6 us; the launch traced here: 10.4 us
  Pallas kernels  9.76 us (92%)
  between operations  0.64 us (6%)
    pallas_call x1, Pallas kernels, per_device(): pl.pallas_call(functools.partial(kernel, lons, lats), out_shape=(out, out...  9.06 us
    pallas_call x1, Pallas kernels, per_device(): pl.pallas_call(store_kernel, out_shape=(jax.ShapeDtypeStruct((columns, ro...  0.7 us

commit v1 on v0

v1 whole, which is shorter than its diff:
```python
import functools

import jax
import jax.numpy as jnp
from jax import lax
from jax.experimental import pallas as pl
from jax.experimental.pallas import tpu as pltpu
from jax.sharding import PartitionSpec as P

COURANT = 0.25
MESH = pl.DeviceIdType.MESH
HIGHEST = lax.Precision.HIGHEST
LAST_WITH_LAST = (((1,), (1,)), ((), ()))
FIRST_WITH_FIRST = (((0,), (0,)), ((), ()))
PLAIN = (((1,), (0,)), ((), ()))
WINDOW = 16
STRIDES = 8


def exact_dot(left, right, dims):
    return lax.dot_general(left, right, dims, precision=HIGHEST, preferred_element_type=jnp.float32)


def pieces(value):
    found = []
    for _ in range(3):
        piece = value.astype(jnp.bfloat16).astype(jnp.float32)
        found.append(piece)
        value = value - piece
    return found


def line_scan(a, lane, upward):
    rows = a.shape[1]
    one, zero = jnp.ones_like(a), jnp.zeros_like(a)

    def behind(v, amount):
        return pltpu.roll(v, amount if upward else rows - amount, 1)

    def inside(amount):
        return lane >= amount if upward else lane < rows - amount

    window = min(WINDOW, rows)
    m = [one, zero, zero, one]
    for i in range(window - 1, -1, -1):
        step = behind(a, i) if i else a
        keep = inside(i)
        for x, y in ((0, 2), (1, 3)):
            total = m[x] + m[y]
            grown = m[x] + step * total
            m[x] = jnp.where(keep, grown, m[x]) if i else grown
            m[y] = jnp.where(keep, total, m[y]) if i else total
    unit = (1.0, 0.0, 0.0, 1.0)
    while window < rows:
        count = min(STRIDES, rows // window)
        terms = [m]
        for i in range(1, count):
            keep = inside(i * window)
            terms.append([jnp.where(keep, behind(v, i * window), u) for v, u in zip(m, unit)])
        while len(terms) > 1:
            joined = []
            for p, q in zip(terms[0::2], terms[1::2]):
                joined.append(
                    [
                        p[0] * q[0] + p[1] * q[2],
                        p[0] * q[1] + p[1] * q[3],
                        p[2] * q[0] + p[3] * q[2],
                        p[2] * q[1] + p[3] * q[3],
                    ]
                )
            terms = joined + terms[2 * len(joined) :]
        m = terms[0]
        window *= count
    return m


def line_factors(a, up, down, before, after, blocks):
    padded, rows = a.shape
    one = jnp.ones_like(a)

    def carried(m, edge, order):
        m = [jnp.broadcast_to(v[:, edge : edge + 1], (padded, rows)) for v in m]
        x, y = one[:1], jnp.zeros_like(one[:1])
        xs, ys, shrink = {}, {}, {}
        for c in order:
            xs[c], ys[c] = x, y
            nx = m[0][c : c + 1] * x + m[1][c : c + 1] * y
            ny = m[2][c : c + 1] * x + m[3][c : c + 1] * y
            ratio = 1.0 / (nx + ny)
            shrink[c] = ratio
            x, y = nx * ratio, ny * ratio
        spare = [one[:1]] * (padded - blocks)
        return [jnp.concatenate([t[c] for c in range(blocks)] + spare, axis=0) for t in (xs, ys, shrink)]

    x_in, y_in, shrink_up = carried(up, rows - 1, range(blocks))
    xb_in, yb_in, shrink_down = carried(down, 0, range(blocks - 1, -1, -1))
    x = up[0] * x_in + up[1] * y_in
    y = up[2] * x_in + up[3] * y_in
    yb = down[2] * xb_in + down[3] * yb_in
    end = lambda v: jnp.broadcast_to(v[:, rows - 1 :], (padded, rows))
    scale = 1.0 / (end(x) + end(y) * xb_in)
    return (
        a * y,
        a * yb,
        y * scale,
        yb * scale,
        shrink_up,
        shrink_down,
        x_in,
        y_in,
        xb_in,
        yb_in,
        -before * y_in,
        after * yb_in,
    )


def kernel(lons, lats, *refs):
    ins, outs, refs = refs[:14], refs[14:17], refs[17:]
    (
        fields,
        land,
        pair,
        wgt,
        slon,
        slat,
        amp,
        factors,
        starts,
        send_lat,
        send_side,
        send_next,
        recv_lat,
        recv_side,
        recv_next,
        recv_sem,
        rim,
        rim_land,
    ) = refs
    a_id = lax.axis_index("lon")
    b_id = lax.axis_index("lat")
    sides = (lax.rem(a_id + lons - 1, lons), lax.rem(a_id + 1, lons))
    znow, depth, hnow, mnow, hold, zold, mold = (fields.at[k] for k in range(7))
    met, cor, samp = pair.at[0], pair.at[1], amp.at[0]
    columns, rows = land.shape
    turns = columns % 128 == 0 and rows % 128 == 0
    padded = wgt.shape[0]

    def early(load_sem, send_sem):
        barrier = pltpu.get_barrier_semaphore()

        def load(group, number, to, at=None):
            source = ins[number] if at is None else ins[number].at[at]
            pltpu.make_async_copy(source, to, load_sem.at[group]).start()

        def loaded(group, ref):
            pltpu.make_async_copy(ref, ref, load_sem.at[group]).wait()

        for k, at in enumerate((0, columns - 1)):
            row = pl.ds(at, 1)
            load(0, 3, rim.at[k, pl.ds(0, 1)], row)
            load(0, 6, rim.at[k, pl.ds(1, 1)], row)
            load(0, 7, rim_land.at[k], row)
            load(0, 1, rim.at[k, pl.ds(2, 1)], row)
        load(1, 8, met)
        load(1, 9, cor)
        load(2, 10, wgt.at[pl.ds(0, lats)])
        load(4, 11, slon)
        load(4, 12, slat)
        load(4, 13, samp)
        for number, slot in ((3, znow), (6, depth), (7, land), (5, mnow), (0, hold), (1, hnow), (2, zold), (4, mold)):
            load(3, number, slot)
        for k in range(1, lats):
            other = lax.rem(b_id + k, lats)
            for column in (*sides, a_id):
                pl.semaphore_signal(barrier, inc=1, device_id=(column, other), device_id_type=MESH)
        for side in sides:
            pl.semaphore_signal(barrier, inc=1, device_id=(side, b_id), device_id_type=MESH)

        loaded(0, rim)
        loaded(1, pair)
        scaled_metric = COURANT * met[...]
        for side, sign in enumerate((-1.0, 1.0)):
            flux = rim[side, 1:2] * rim_land[side].astype(jnp.float32) * rim[side, 0:1]
            flux = sign * scaled_metric * flux
            send_side[side] = flux
            send_next[side] = jnp.concatenate([flux, rim[side, 2:3]], axis=0)

        def remote(src, dst, kind, column, row):
            return pltpu.make_async_remote_copy(
                src_ref=src,
                dst_ref=dst,
                send_sem=send_sem.at[kind],
                recv_sem=recv_sem.at[kind],
                device_id=(column, row),
                device_id_type=MESH,
            )

        def greet_and_send_edges():
            pl.semaphore_wait(barrier, 3 * lats - 1)
            for k in range(1, lats):
                for side in (1, 0):
                    remote(
                        send_side.at[side],
                        recv_side.at[side, lats - k - 1],
                        0,
                        sides[side],
                        lax.rem(b_id + k, lats),
                    ).start()
            for side in (0, 1):
                remote(send_next.at[side], recv_next.at[side], 1, sides[side], b_id).start()

        far = jnp.logical_and(b_id == lats - 1, a_id > 1)
        pl.when(far)(greet_and_send_edges)

        loaded(2, wgt.at[pl.ds(0, lats)])
        loaded(4, amp)
        sources = slon.shape[1]
        east_cell = lax.broadcasted_iota(jnp.int32, (columns, sources), 0) + a_id * columns
        north_cell = lax.broadcasted_iota(jnp.int32, (rows, sources), 0) + b_id * rows
        hit_east = east_cell == slon[...]
        hit_north = jnp.where(north_cell == slat[...], 1.0, 0.0).astype(jnp.bfloat16)
        added = [
            lax.dot_general(
                jnp.where(hit_east, piece, 0.0).astype(jnp.bfloat16),
                hit_north,
                LAST_WITH_LAST,
                preferred_element_type=jnp.float32,
            )
            for piece in pieces(samp[...])
        ]
        added = added[0] + added[1] + added[2]
        weight = wgt[...]
        if padded > lats:
            row_id = lax.broadcasted_iota(jnp.int32, (padded, rows), 0)
            weight = jnp.where(row_id < lats, weight, 1.0)
        a = 1.0 / weight
        lane_of = lax.broadcasted_iota(jnp.int32, (padded, rows), 1)
        first_lane, last_lane = lane_of == 0, lane_of == rows - 1
        before = COURANT * pltpu.roll(jnp.broadcast_to(a[:, rows - 1 :], (padded, rows)), 1, 0)
        after = COURANT * pltpu.roll(jnp.broadcast_to(a[:, :1], (padded, rows)), padded - 1, 0)
        up = line_scan(a, lane_of, True)
        down = line_scan(a, lane_of, False)
        zeros = jnp.zeros_like(a)
        at_last = lambda v: jnp.where(last_lane, v, zeros)
        at_first = lambda v: jnp.where(first_lane, v, zeros)
        for k, value in enumerate(
            (
                a * up[2],
                a * up[3],
                a * down[2],
                a * down[3],
                at_last((up[0] + up[2]) * after),
                at_last((up[1] + up[3]) * after) - at_first(before),
                -at_first((down[0] + down[2]) * before),
                at_last(after) - at_first((down[1] + down[3]) * before),
            )
        ):
            starts[k] = value

        loaded(3, fields)
        wet = land[...].astype(jnp.float32)
        wet_depth = depth[...] * wet
        flux_east = wet_depth * znow[...]
        flux_north = wet_depth * mnow[...]
        metric = met[...]
        line = lax.broadcasted_iota(jnp.int32, (columns, rows), 0)
        lane = lax.broadcasted_iota(jnp.int32, (columns, rows), 1)

        def inner_diff(v, axis, position, size):
            ahead = jnp.where(position == size - 1, 0.0, pltpu.roll(v, size - 1, axis))
            behind = jnp.where(position == 0, 0.0, pltpu.roll(v, 1, axis))
            return ahead - behind

        rhs = added + hold[...] - COURANT * (
            metric * inner_diff(flux_east, 0, line, columns) + inner_diff(flux_north, 1, lane, rows)
        )
        height = hnow[...]
        row_lane = lax.broadcasted_iota(jnp.int32, (1, rows), 1)
        first_row = jnp.where(row_lane == 0, 1.0, 0.0)
        last_row = jnp.where(row_lane == rows - 1, 1.0, 0.0)
        zero_row = jnp.zeros((1, rows), jnp.float32)
        outer = exact_dot(
            jnp.concatenate([zero_row, zero_row, last_row, zero_row] + [zero_row] * 2 + [first_row, zero_row], axis=0),
            height,
            LAST_WITH_LAST,
        )
        def start(k):
            return starts[k, pl.ds(b_id, 1), :]

        def laid(k):
            return jnp.concatenate(
                [start(k), start(k + 1), zero_row, zero_row, start(k + 2), start(k + 3), zero_row, zero_row], axis=0
            )

        moments = outer + exact_dot(
            jnp.concatenate([laid(0), laid(4)], axis=1),
            jnp.concatenate([rhs, flux_north], axis=1),
            LAST_WITH_LAST,
        )
        send_lat[0] = moments[0:4]
        send_lat[1] = moments[4:8]
        pl.when(jnp.logical_not(far))(greet_and_send_edges)
        for k in range(1, lats):
            remote(
                send_lat.at[jnp.where(b_id + k < lats, 0, 1)],
                recv_lat.at[lats - k - 1],
                2,
                a_id,
                lax.rem(b_id + k, lats),
            ).start()

        ends = exact_dot(
            jnp.concatenate([first_row, last_row] + [zero_row] * 6, axis=0), flux_north, LAST_WITH_LAST
        )

        for k, value in enumerate(line_factors(a, up, down, before, after, lats)):
            factors[k] = value

        def own(k, block):
            return factors[k, pl.ds(block, 1), :]

        ay, ayb, y_s, yb_s = [own(k, b_id) for k in range(4)]
        columns_of = jnp.transpose(jnp.concatenate([ay, ayb, yb_s, y_s] + [zero_row] * 4, axis=0))
        source_lat = lax.broadcasted_iota(jnp.int32, (rows, rows), 0)
        target_lat = lax.broadcasted_iota(jnp.int32, (rows, rows), 1)
        below = source_lat <= target_lat
        inverse = jnp.where(below, columns_of[:, 0:1] * yb_s, columns_of[:, 1:2] * y_s)
        outs[0][...] = exact_dot(rhs, inverse, PLAIN)
        turning = cor[...]
        outs[1][...] = wet * (
            zold[...] + turning * mnow[...] - COURANT * metric * inner_diff(height, 0, line, columns)
        )
        outs[2][...] = mold[...] - COURANT * inner_diff(height, 1, lane, rows) - turning * znow[...]

        def across(v):
            return v[:, :columns] if columns <= rows else jnp.broadcast_to(v[:, :1], (1, columns))

        coarse, fine, reach = [None] * lats, [None] * lats, [None] * lats
        product = jnp.ones((1, rows), jnp.float32)
        for d in range(lats - 1, 0, -1):
            block = lax.rem(b_id + d, lats)
            product = product * own(4, block)
            coarse[d], fine[d], reach[d] = own(6, block) * product, own(7, block) * product, own(0, block) * product
        product = jnp.ones((1, rows), jnp.float32)
        for d in range(1, lats):
            block = lax.rem(b_id + d, lats)
            north = b_id + d < lats
            product = product * own(5, block)
            coarse[d] = jnp.where(north, own(8, block) * product, coarse[d])
            fine[d] = jnp.where(north, own(9, block) * product, fine[d])
            reach[d] = jnp.where(north, own(1, block) * product, reach[d])
        own_low = across(own(10, b_id)) * ends[0:1]
        own_high = across(own(11, b_id)) * ends[1:2]
        if turns:
            basis = [jnp.broadcast_to(columns_of[:, k : k + 1], (rows, columns)) for k in (2, 3)]
        else:
            basis = pieces(
                jnp.concatenate(
                    [
                        jnp.concatenate([yb_s, y_s] + [zero_row] * 6, axis=0),
                        jnp.concatenate([zero_row, zero_row, COURANT * first_row, -COURANT * last_row] + [zero_row] * 4, axis=0),
                    ],
                    axis=1,
                )
            )
            basis = jnp.concatenate([basis[k] for k in (0, 1, 2, 0, 1, 0)], axis=0).astype(jnp.bfloat16)
        full = jnp.ones((rows, rows), jnp.float32)
        lower = jnp.where(below, 1.0, 0.0)
        running = jnp.concatenate(
            [jnp.concatenate([lower, full], axis=0), jnp.concatenate([1.0 - lower, full], axis=0)], axis=1
        ).astype(jnp.bfloat16)

        for kind, ref in enumerate((recv_side, recv_next, recv_lat)):
            pltpu.make_async_copy(ref, ref, send_sem.at[kind]).wait()
        return coarse[1:], fine[1:], reach[1:], own_low, own_high, basis, running, ay, ayb, y_s, yb_s

    coarse, fine, reach, own_low, own_high, basis, running, ay, ayb, y_s, yb_s = pl.run_scoped(
        early, pltpu.SemaphoreType.DMA((5,)), pltpu.SemaphoreType.DMA((3,))
    )
    coarse, fine, reach = [None, *coarse], [None, *fine], [None, *reach]

    def across(v):
        return v[:, :columns] if columns <= rows else jnp.broadcast_to(v[:, :1], (1, columns))

    zero_row = jnp.zeros((1, rows), jnp.float32)
    wet, metric = land[...].astype(jnp.float32), met[...]
    arrivals = ((2, recv_lat), (1, recv_next), (0, recv_side))
    for kind, ref in arrivals:
        pltpu.make_async_copy(ref, ref, recv_sem.at[kind]).wait()

    low, high = own_low, own_high
    for d in range(1, lats):
        arrived = recv_lat[d - 1, 0:1] * across(coarse[d]) + recv_lat[d - 1, 1:2] * across(fine[d])
        north = b_id + d < lats
        high = high + jnp.where(north, arrived, 0.0)
        low = low + jnp.where(north, 0.0, arrived)
    south_height = jnp.where(b_id > 0, recv_lat[lats - 2, 2:3], 0.0)
    north_height = jnp.where(b_id < lats - 1, recv_lat[0, 2:3], 0.0)
    if turns:
        lat_at = lax.broadcasted_iota(jnp.int32, (rows, columns), 0)
        outside = jnp.where(
            lat_at == 0, COURANT * south_height, jnp.where(lat_at == rows - 1, -COURANT * north_height, 0.0)
        )
        height_term = jnp.transpose(basis[0] * low + basis[1] * high)
        velocity_term = jnp.transpose(outside)
    else:
        carried = pieces(
            jnp.concatenate([low, high, south_height, north_height, jnp.zeros((4, columns), jnp.float32)], axis=0)
        )
        carried = jnp.concatenate([carried[k] for k in (0, 0, 0, 1, 1, 2)], axis=0).astype(jnp.bfloat16)
        corrections = lax.dot_general(carried, basis, FIRST_WITH_FIRST, preferred_element_type=jnp.float32)
        height_term, velocity_term = corrections[:, :rows], corrections[:, rows:]

    lows, highs = [], []
    for side in (1, 0):
        flux = recv_next[side, 0:1]
        low, high = zero_row, zero_row
        for d in range(1, lats):
            arrived = recv_side[side, d - 1] * reach[d]
            north = b_id + d < lats
            high = high + jnp.where(north, arrived, 0.0)
            low = low + jnp.where(north, 0.0, arrived)
        lows.append(jnp.concatenate([flux * ay, low], axis=1))
        highs.append(jnp.concatenate([flux * ayb, high], axis=1))
    spare = jnp.zeros((4, 2 * rows), jnp.float32)
    edges = jnp.concatenate(pieces(jnp.concatenate(lows + highs + [spare], axis=0)), axis=0)
    edges = jnp.concatenate([edges, jnp.zeros((8, 2 * rows), jnp.float32)], axis=0).astype(jnp.bfloat16)
    edges = lax.dot_general(edges, running, PLAIN, preferred_element_type=jnp.float32)
    edges = edges[0:8] + edges[8:16] + edges[16:24]

    solved = outs[0][...] + height_term
    outs[0][...] = wet * solved
    outs[2][...] = wet * (outs[2][...] + velocity_term)
    for k, (at, side, sign) in enumerate(((0, 1, COURANT), (columns - 1, 0, -COURANT))):
        edge = pl.ds(at, 1)
        outs[0][edge, :] = wet[at : at + 1] * (
            solved[at : at + 1] + edges[k : k + 1, :rows] * yb_s + edges[2 + k : 3 + k, rows:] * y_s
        )
        outs[1][edge, :] = outs[1][edge, :] + wet[at : at + 1] * (sign * metric * recv_next[side, 1:2])


def store_kernel(*refs):
    stores = [
        pltpu.make_async_copy(refs[k], refs[3 + k], refs[6].at[k]) for k in range(3)
    ]
    for store in stores:
        store.start()
    for store in stores:
        store.wait()


def per_device(lons, lats, *args):
    args = list(args)
    columns, rows = args[0].shape
    sources = args[11].shape[0]
    padded = -(-lats // 8) * 8
    args[8] = args[8].reshape(1, rows)
    args[9] = args[9].reshape(1, rows)
    args[10] = args[10].reshape(lats, rows)
    for k in (11, 12, 13):
        args[k] = args[k].reshape(1, sources)
    out = pltpu.VMEM((columns, rows), jnp.float32)
    others = lats - 1
    results = pl.pallas_call(
        functools.partial(kernel, lons, lats),
        out_shape=(out, out, out),
        in_specs=[pl.BlockSpec(memory_space=pl.ANY)] * 14,
        out_specs=(pl.BlockSpec(memory_space=pltpu.VMEM),) * 3,
        scratch_shapes=[
            pltpu.VMEM((8, columns, rows), jnp.float32),
            pltpu.VMEM((columns, rows), jnp.int32),
            pltpu.VMEM((2, 1, rows), jnp.float32),
            pltpu.VMEM((padded, rows), jnp.float32),
            pltpu.VMEM((1, sources), jnp.int32),
            pltpu.VMEM((1, sources), jnp.int32),
            pltpu.VMEM((3, 1, sources), jnp.float32),
            pltpu.VMEM((12, padded, rows), jnp.float32),
            pltpu.VMEM((8, padded, rows), jnp.float32),
            pltpu.VMEM((2, 4, columns), jnp.float32),
            pltpu.VMEM((2, 1, rows), jnp.float32),
            pltpu.VMEM((2, 2, rows), jnp.float32),
            pltpu.VMEM((others, 4, columns), jnp.float32),
            pltpu.VMEM((2, others, 1, rows), jnp.float32),
            pltpu.VMEM((2, 2, rows), jnp.float32),
            pltpu.SemaphoreType.DMA((3,)),
            pltpu.VMEM((2, 4, rows), jnp.float32),
            pltpu.VMEM((2, 1, rows), jnp.int32),
        ],
        compiler_params=pltpu.CompilerParams(collective_id=0, has_side_effects=True),
    )(*args)
    return pl.pallas_call(
        store_kernel,
        out_shape=(jax.ShapeDtypeStruct((columns, rows), jnp.float32),) * 3,
        in_specs=[pl.BlockSpec(memory_space=pltpu.VMEM)] * 3,
        out_specs=(pl.BlockSpec(memory_space=pl.ANY),) * 3,
        scratch_shapes=[pltpu.SemaphoreType.DMA((3,))],
    )(*[pltpu.with_memory_space_constraint(r, pltpu.VMEM) for r in results])


def solution(mesh):
    field = P("lon", "lat")
    placed = (field,) * 8 + (P("lat"),) * 2 + (P(),) * 4
    return jax.shard_map(
        functools.partial(per_device, mesh.shape["lon"], mesh.shape["lat"]),
        mesh=mesh,
        in_specs=placed,
        out_specs=(field,) * 3,
        check_vma=False,
    )
```

time: 10.6 us -> 10.5 us (level)
  Pallas kernels: 9.76 us -> 9.63 us
    pallas_call x1, Pallas kernels: 9.06 us -> 8.93 us  [per_device(): pl.pallas_call(functools.partial(kernel, lons, lats), out_shape=(out, out...]
where the time goes in v1:
time: 10.5 us; the launch traced here: 10.3 us
  Pallas kernels  9.63 us (92%)
  between operations  0.64 us (6%)
    pallas_call x1, Pallas kernels, per_device(): pl.pallas_call(functools.partial(kernel, lons, lats), out_shape=(out, out...  8.93 us
    pallas_call x1, Pallas kernels, per_device(): pl.pallas_call(store_kernel, out_shape=(jax.ShapeDtypeStruct((columns, ro...  0.7 us

profile of v1, /device:TPU:0, one launch (start us, length us, event | category | flops | bytes accessed | tf_op | source)
XLA Modules:
  0.0 10.3 jit_solution(13474224739317032568)
XLA Ops:
  0.6 8.9 %shard_map.157 = (f32[128,128]{1,0:T(8,128)S(1)}, f32[128,128]{1,0:T(8,128)S(1)}, f32[128,128]{1,0:T(8,128)S(1)}) custom-call(f32[128,128]{1,0:T(8,128)} %refs_0_.1, f32[128,128]{1,0:T(8,128)} %refs_1_.1, f32[128,128]{1,0:T(8,128)} %refs_2_.1, f32[128,128]{1,0:T(8,128)} %refs_3_.1, f32[128,128]{1,0:T(8,128)} %refs_4_.1, f32[128,128]{1,0:T(8,128)} %refs_5_.1, ...), custom_call_target="tpu_custom_call" | custom-call | tf_op jit(solution)/shard_map/pallas_call | solution.py:465
  9.6 0.7 %shard_map.158 = (f32[128,128]{1,0:T(8,128)}, f32[128,128]{1,0:T(8,128)}, f32[128,128]{1,0:T(8,128)}) custom-call(f32[128,128]{1,0:T(8,128)S(1)} %get-tuple-element.6.refs_0_, f32[128,128]{1,0:T(8,128)S(1)} %get-tuple-element.7.refs_1_, f32[128,128]{1,0:T(8,128)S(1)} %get-tuple-element.8.refs_2_), custom_call_target="tpu_custom_call" | custom-call | tf_op jit(solution)/shard_map/pallas_call | solution.py:492

commit v2 on v1

--- a/solution.py
+++ b/solution.py
@@ -143,6 +143,12 @@
     znow, depth, hnow, mnow, hold, zold, mold = (fields.at[k] for k in range(7))
     met, cor, samp = pair.at[0], pair.at[1], amp.at[0]
     columns, rows = land.shape
+    trims = lats >= 4 and lats % 2 == 0
+    lat_bytes = recv_lat.at[pl.ds(0, lats // 2)] if trims else recv_lat
+
+    def part(k):
+        return pl.ds(0, (3 if k in (1, lats - 1) else 2) if trims else 4)
+
     turns = columns % 128 == 0 and rows % 128 == 0
     padded = wgt.shape[0]
 
@@ -303,8 +309,8 @@
         pl.when(jnp.logical_not(far))(greet_and_send_edges)
         for k in range(1, lats):
             remote(
-                send_lat.at[jnp.where(b_id + k < lats, 0, 1)],
-                recv_lat.at[lats - k - 1],
+                send_lat.at[jnp.where(b_id + k < lats, 0, 1), part(k)],
+                recv_lat.at[lats - k - 1, part(k)],
                 2,
                 a_id,
                 lax.rem(b_id + k, lats),
@@ -371,7 +377,7 @@
             [jnp.concatenate([lower, full], axis=0), jnp.concatenate([1.0 - lower, full], axis=0)], axis=1
         ).astype(jnp.bfloat16)
 
-        for kind, ref in enumerate((recv_side, recv_next, recv_lat)):
+        for kind, ref in enumerate((recv_side, recv_next, lat_bytes)):
             pltpu.make_async_copy(ref, ref, send_sem.at[kind]).wait()
         return coarse[1:], fine[1:], reach[1:], own_low, own_high, basis, running, ay, ayb, y_s, yb_s
 
@@ -385,7 +391,7 @@
 
     zero_row = jnp.zeros((1, rows), jnp.float32)
     wet, metric = land[...].astype(jnp.float32), met[...]
-    arrivals = ((2, recv_lat), (1, recv_next), (0, recv_side))
+    arrivals = ((1, recv_next), (0, recv_side), (2, lat_bytes))
     for kind, ref in arrivals:
         pltpu.make_async_copy(ref, ref, recv_sem.at[kind]).wait()
 
@@ -441,13 +447,14 @@
 
 
 def store_kernel(*refs):
-    stores = [
-        pltpu.make_async_copy(refs[k], refs[3 + k], refs[6].at[k]) for k in range(3)
-    ]
-    for store in stores:
-        store.start()
-    for store in stores:
-        store.wait()
+    def move(sem):
+        stores = [pltpu.make_async_copy(refs[k], refs[3 + k], sem.at[k]) for k in range(3)]
+        for store in stores:
+            store.start()
+        for store in stores:
+            store.wait()
+
+    pl.run_scoped(move, pltpu.SemaphoreType.DMA((3,)))
 
 
 def per_device(lons, lats, *args):
@@ -494,7 +501,6 @@
         out_shape=(jax.ShapeDtypeStruct((columns, rows), jnp.float32),) * 3,
         in_specs=[pl.BlockSpec(memory_space=pltpu.VMEM)] * 3,
         out_specs=(pl.BlockSpec(memory_space=pl.ANY),) * 3,
-        scratch_shapes=[pltpu.SemaphoreType.DMA((3,))],
     )(*[pltpu.with_memory_space_constraint(r, pltpu.VMEM) for r in results])
 
 

time: 10.5 us -> 10.4 us (level)
  no operation moved by 1% of the time
where the time goes in v2:
time: 10.4 us; the launch traced here: 10.2 us
  Pallas kernels  9.57 us (92%)
  between operations  0.64 us (6%)
    pallas_call x1, Pallas kernels, per_device(): pl.pallas_call(functools.partial(kernel, lons, lats), out_shape=(out, out...  8.9 us
    pallas_call x1, Pallas kernels, per_device(): pl.pallas_call(store_kernel, out_shape=(jax.ShapeDtypeStruct((columns, ro...  0.67 us

profile of v2, /device:TPU:0, one launch (start us, length us, event | category | flops | bytes accessed | tf_op | source)
XLA Modules:
  0.0 10.2 jit_solution(18026821857096405225)
XLA Ops:
  0.6 8.9 %shard_map.157 = (f32[128,128]{1,0:T(8,128)S(1)}, f32[128,128]{1,0:T(8,128)S(1)}, f32[128,128]{1,0:T(8,128)S(1)}) custom-call(f32[128,128]{1,0:T(8,128)} %refs_0_.1, f32[128,128]{1,0:T(8,128)} %refs_1_.1, f32[128,128]{1,0:T(8,128)} %refs_2_.1, f32[128,128]{1,0:T(8,128)} %refs_3_.1, f32[128,128]{1,0:T(8,128)} %refs_4_.1, f32[128,128]{1,0:T(8,128)} %refs_5_.1, ...), custom_call_target="tpu_custom_call" | custom-call | tf_op jit(solution)/shard_map/pallas_call | solution.py:472
  9.5 0.7 %shard_map.158 = (f32[128,128]{1,0:T(8,128)}, f32[128,128]{1,0:T(8,128)}, f32[128,128]{1,0:T(8,128)}) custom-call(f32[128,128]{1,0:T(8,128)S(1)} %get-tuple-element.6.refs_0_, f32[128,128]{1,0:T(8,128)S(1)} %get-tuple-element.7.refs_1_, f32[128,128]{1,0:T(8,128)S(1)} %get-tuple-element.8.refs_2_), custom_call_target="tpu_custom_call" | custom-call | tf_op jit(solution)/shard_map/pallas_call | solution.py:499

commit v3 on v2

--- a/solution.py
+++ b/solution.py
@@ -174,14 +174,19 @@
         load(4, 11, slon)
         load(4, 12, slat)
         load(4, 13, samp)
+        south_half = 2 * b_id < lats
+        for k in range(lats - 1):
+            down, up_row = lats - 1 - k, k
+            down = down - (down <= b_id).astype(jnp.int32)
+            up_row = up_row + (up_row >= b_id).astype(jnp.int32)
+            other = jnp.where(south_half, down, up_row)
+            for column in (*sides, a_id):
+                pl.semaphore_signal(barrier, inc=1, device_id=(column, other), device_id_type=MESH)
+            if k == 0:
+                for side in sides:
+                    pl.semaphore_signal(barrier, inc=1, device_id=(side, b_id), device_id_type=MESH)
         for number, slot in ((3, znow), (6, depth), (7, land), (5, mnow), (0, hold), (1, hnow), (2, zold), (4, mold)):
             load(3, number, slot)
-        for k in range(1, lats):
-            other = lax.rem(b_id + k, lats)
-            for column in (*sides, a_id):
-                pl.semaphore_signal(barrier, inc=1, device_id=(column, other), device_id_type=MESH)
-        for side in sides:
-            pl.semaphore_signal(barrier, inc=1, device_id=(side, b_id), device_id_type=MESH)
 
         loaded(0, rim)
         loaded(1, pair)

time: 10.4 us -> 10.4 us (level)
  no operation moved by 1% of the time
where the time goes in v3:
time: 10.4 us; the launch traced here: 10.2 us
  Pallas kernels  9.53 us (92%)
  between operations  0.64 us (6%)
    pallas_call x1, Pallas kernels, per_device(): pl.pallas_call(functools.partial(kernel, lons, lats), out_shape=(out, out...  8.86 us
    pallas_call x1, Pallas kernels, per_device(): pl.pallas_call(store_kernel, out_shape=(jax.ShapeDtypeStruct((columns, ro...  0.67 us

profile of v3, /device:TPU:0, one launch (start us, length us, event | category | flops | bytes accessed | tf_op | source)
XLA Modules:
  0.0 10.2 jit_solution(5933315866811068699)
XLA Ops:
  0.6 8.9 %shard_map.157 = (f32[128,128]{1,0:T(8,128)S(1)}, f32[128,128]{1,0:T(8,128)S(1)}, f32[128,128]{1,0:T(8,128)S(1)}) custom-call(f32[128,128]{1,0:T(8,128)} %refs_0_.1, f32[128,128]{1,0:T(8,128)} %refs_1_.1, f32[128,128]{1,0:T(8,128)} %refs_2_.1, f32[128,128]{1,0:T(8,128)} %refs_3_.1, f32[128,128]{1,0:T(8,128)} %refs_4_.1, f32[128,128]{1,0:T(8,128)} %refs_5_.1, ...), custom_call_target="tpu_custom_call" | custom-call | tf_op jit(solution)/shard_map/pallas_call | solution.py:477
  9.5 0.7 %shard_map.158 = (f32[128,128]{1,0:T(8,128)}, f32[128,128]{1,0:T(8,128)}, f32[128,128]{1,0:T(8,128)}) custom-call(f32[128,128]{1,0:T(8,128)S(1)} %get-tuple-element.6.refs_0_, f32[128,128]{1,0:T(8,128)S(1)} %get-tuple-element.7.refs_1_, f32[128,128]{1,0:T(8,128)S(1)} %get-tuple-element.8.refs_2_), custom_call_target="tpu_custom_call" | custom-call | tf_op jit(solution)/shard_map/pallas_call | solution.py:504

commit v4 on v3

--- a/solution.py
+++ b/solution.py
@@ -207,22 +207,33 @@
                 device_id_type=MESH,
             )
 
-        def greet_and_send_edges():
+        def send_moments(k):
+            remote(
+                send_lat.at[jnp.where(b_id + k < lats, 0, 1), part(k)],
+                recv_lat.at[lats - k - 1, part(k)],
+                2,
+                a_id,
+                lax.rem(b_id + k, lats),
+            ).start()
+
+        def greet_and_send(moments_too):
             pl.semaphore_wait(barrier, 3 * lats - 1)
+            if moments_too:
+                send_moments(1)
             for k in range(1, lats):
+                row = k - 1 + (b_id <= k - 1).astype(jnp.int32)
+                slot = lats - 2 - lax.rem(row - b_id + lats - 1, lats)
                 for side in (1, 0):
-                    remote(
-                        send_side.at[side],
-                        recv_side.at[side, lats - k - 1],
-                        0,
-                        sides[side],
-                        lax.rem(b_id + k, lats),
-                    ).start()
-            for side in (0, 1):
-                remote(send_next.at[side], recv_next.at[side], 1, sides[side], b_id).start()
-
-        far = jnp.logical_and(b_id == lats - 1, a_id > 1)
-        pl.when(far)(greet_and_send_edges)
+                    remote(send_side.at[side], recv_side.at[side, slot], 0, sides[side], row).start()
+                if k == 1:
+                    for side in (1, 0):
+                        remote(send_next.at[side], recv_next.at[side], 1, sides[side], b_id).start()
+            if moments_too:
+                for k in range(2, lats):
+                    send_moments(k)
+
+        far = jnp.logical_and(2 * b_id >= lats, a_id > 1)
+        pl.when(far)(lambda: greet_and_send(False))
 
         loaded(2, wgt.at[pl.ds(0, lats)])
         loaded(4, amp)
@@ -311,15 +322,14 @@
         )
         send_lat[0] = moments[0:4]
         send_lat[1] = moments[4:8]
-        pl.when(jnp.logical_not(far))(greet_and_send_edges)
-        for k in range(1, lats):
-            remote(
-                send_lat.at[jnp.where(b_id + k < lats, 0, 1), part(k)],
-                recv_lat.at[lats - k - 1, part(k)],
-                2,
-                a_id,
-                lax.rem(b_id + k, lats),
-            ).start()
+        @pl.when(jnp.logical_not(far))
+        def _():
+            greet_and_send(True)
+
+        @pl.when(far)
+        def _():
+            for k in range(1, lats):
+                send_moments(k)
 
         ends = exact_dot(
             jnp.concatenate([first_row, last_row] + [zero_row] * 6, axis=0), flux_north, LAST_WITH_LAST

time: 10.4 us -> 10.4 us (level)
  no operation moved by 1% of the time
where the time goes in v4:
time: 10.4 us; the launch traced here: 10.2 us
  Pallas kernels  9.53 us (92%)
  between operations  0.64 us (6%)
    pallas_call x1, Pallas kernels, per_device(): pl.pallas_call(functools.partial(kernel, lons, lats), out_shape=(out, out...  8.85 us
    pallas_call x1, Pallas kernels, per_device(): pl.pallas_call(store_kernel, out_shape=(jax.ShapeDtypeStruct((columns, ro...  0.67 us

profile of v4, /device:TPU:0, one launch (start us, length us, event | category | flops | bytes accessed | tf_op | source)
XLA Modules:
  0.0 10.2 jit_solution(10775260895877696526)
XLA Ops:
  0.6 8.9 %shard_map.157 = (f32[128,128]{1,0:T(8,128)S(1)}, f32[128,128]{1,0:T(8,128)S(1)}, f32[128,128]{1,0:T(8,128)S(1)}) custom-call(f32[128,128]{1,0:T(8,128)} %refs_0_.1, f32[128,128]{1,0:T(8,128)} %refs_1_.1, f32[128,128]{1,0:T(8,128)} %refs_2_.1, f32[128,128]{1,0:T(8,128)} %refs_3_.1, f32[128,128]{1,0:T(8,128)} %refs_4_.1, f32[128,128]{1,0:T(8,128)} %refs_5_.1, ...), custom_call_target="tpu_custom_call" | custom-call | tf_op jit(solution)/shard_map/pallas_call | solution.py:487
  9.5 0.7 %shard_map.158 = (f32[128,128]{1,0:T(8,128)}, f32[128,128]{1,0:T(8,128)}, f32[128,128]{1,0:T(8,128)}) custom-call(f32[128,128]{1,0:T(8,128)S(1)} %get-tuple-element.6.refs_0_, f32[128,128]{1,0:T(8,128)S(1)} %get-tuple-element.7.refs_1_, f32[128,128]{1,0:T(8,128)S(1)} %get-tuple-element.8.refs_2_), custom_call_target="tpu_custom_call" | custom-call | tf_op jit(solution)/shard_map/pallas_call | solution.py:514
